TPU v7x, 32 devices: a whole 2x2x4 slice. The times are simulated.
32 devices in a mesh: row: 16 (over z, x, core), col: 2 (over y).
Axes of the slice: x: 2, y: 2, z: 4, core: 2. Of those that a mesh axis runs over, the one named last changes fastest.
Arguments:
- sequence_embedding: float32 [128, 64, 256], P('row', 'col'), may hold values from -6 to 6
- standardize_scale: float32 [256], replicated, may hold values from 0.25 to 1.75
- standardize_offset: float32 [256], replicated, may hold values from -0.5 to 0.5
- first_operand_matrix: float32 [256, 32], replicated, may hold values from -0.375 to 0.375
- first_operand_intercept: float32 [32], replicated, may hold values from -0.5 to 0.5
- second_operand_matrix: float32 [256, 32], replicated, may hold values from -0.375 to 0.375
- second_operand_intercept: float32 [32], replicated, may hold values from -0.5 to 0.5
- result_matrix: float32 [1024, 128], replicated, may hold values from -2 to 2
- result_intercept: float32 [128], replicated, may hold values from -0.5 to 0.5
- edge_incoming_sensitivity: float32 [64, 64, 128], P('row', 'col'), may hold values from -6 to 6
Outputs:
- pair_output_update: float32 [64, 64, 128], P('row', 'col')
- alignment_gradient: float32 [128, 64, 256], P('row', 'col')
- projection_gradient: float32 [1024, 128], P(('row', 'col'))
All inputs are finite; a program needn't handle non-finite values.
Results may differ from a plain program's by a relative error of at most 0.0001.
Values sent between devices are 32-bit elements; how exact they have to be, the bound alone decides.
A program may use at most 64 MiB of HBM per device.

v0:
```python
import math

import jax
import jax.numpy as jnp
from jax import lax
from jax.sharding import PartitionSpec as P

precise = lax.Precision.HIGHEST


def linear_transform(
    sequence_embedding,
    standardize_scale,
    standardize_offset,
    first_operand_matrix,
    first_operand_intercept,
    second_operand_matrix,
    second_operand_intercept,
):
    average_feature = jnp.mean(sequence_embedding, axis=-1, keepdims=True)
    demeaned_features = sequence_embedding - average_feature
    variance = jnp.mean(demeaned_features * demeaned_features, axis=-1, keepdims=True)
    normed = (
        demeaned_features * lax.rsqrt(variance + 1e-05) * standardize_scale + standardize_offset
    )
    first_operand_entries = (
        jnp.einsum("src,cd->srd", normed, first_operand_matrix, precision=precise)
        + first_operand_intercept
    )
    second_operand_entries = (
        jnp.einsum("src,cd->srd", normed, second_operand_matrix, precision=precise)
        + second_operand_intercept
    )
    return (first_operand_entries, second_operand_entries)


def tile_work(left_all, right_all, result_matrix, result_intercept, edge_incoming_sensitivity):
    rows_all, tile_i, chans = left_all.shape
    tile_j = right_all.shape[1]
    pair_ch = result_matrix.shape[1]
    block_rows = math.gcd(tile_i, 8)
    num_blocks = tile_i // block_rows
    left_blocks = left_all.reshape(rows_all, num_blocks, block_rows, chans).transpose(1, 0, 2, 3)
    cot_blocks = edge_incoming_sensitivity.reshape(num_blocks, block_rows, tile_j, pair_ch)

    def tile_step(carry, inputs):
        summed_weight, right_sum = carry
        left_blk, cot_blk = inputs
        products = jnp.einsum("sic,sje->ijce", left_blk, right_all, precision=precise)
        products = products.reshape(block_rows, tile_j, chans * chans)
        pair_blk = (
            jnp.einsum("ijk,kh->ijh", products, result_matrix, precision=precise) / rows_all
            + result_intercept
        )
        grad_outer = jnp.einsum("ijh,kh->ijk", cot_blk, result_matrix, precision=precise) / rows_all
        grad_outer = grad_outer.reshape(block_rows, tile_j, chans, chans)
        summed_weight = summed_weight + jnp.einsum(
            "ijk,ijh->kh", products, cot_blk, precision=precise
        )
        left_factor_gradient = jnp.einsum("ijce,sje->sic", grad_outer, right_all, precision=precise)
        right_sum = right_sum + jnp.einsum("sic,ijce->sje", left_blk, grad_outer, precision=precise)
        return ((summed_weight, right_sum), (pair_blk, left_factor_gradient))

    initial = (
        jnp.zeros((chans * chans, pair_ch), jnp.float32),
        jnp.zeros(right_all.shape, jnp.float32),
    )
    (summed_weight, right_sum), (pair_blocks, left_grads) = lax.scan(
        tile_step, initial, (left_blocks, cot_blocks)
    )
    pair_tile = pair_blocks.reshape(tile_i, tile_j, pair_ch)
    left_factor_gradient = left_grads.transpose(1, 0, 2, 3).reshape(rows_all, tile_i, chans)
    return (pair_tile, left_factor_gradient, summed_weight, right_sum)


def local(
    sequence_embedding,
    standardize_scale,
    standardize_offset,
    first_operand_matrix,
    first_operand_intercept,
    second_operand_matrix,
    second_operand_intercept,
    result_matrix,
    result_intercept,
    edge_incoming_sensitivity,
):

    def device_portion(values):
        return linear_transform(
            values,
            standardize_scale,
            standardize_offset,
            first_operand_matrix,
            first_operand_intercept,
            second_operand_matrix,
            second_operand_intercept,
        )

    (first_operand_portion, second_operand_portion), reverse_derivative = jax.vjp(
        device_portion, sequence_embedding
    )
    col_count = lax.axis_size("col")
    right_all = lax.all_gather(second_operand_portion, "row", axis=0, tiled=True)
    widened = lax.all_gather(first_operand_portion, "col", axis=1, tiled=True)
    left_all = lax.all_to_all(widened, "row", split_axis=1, concat_axis=0, tiled=True)
    pair_output_update, left_factor_gradient, summed_weight, right_sum = tile_work(
        left_all, right_all, result_matrix, result_intercept, edge_incoming_sensitivity
    )
    swapped = lax.all_to_all(left_factor_gradient, "row", split_axis=0, concat_axis=1, tiled=True)
    left_backprop = lax.psum_scatter(swapped, "col", scatter_dimension=1, tiled=True)
    right_backprop = lax.psum_scatter(right_sum, "row", scatter_dimension=0, tiled=True)
    alignment_gradient = reverse_derivative((left_backprop, right_backprop))[0]
    res_total = right_all.shape[1] * col_count
    projection_gradient = (
        lax.psum_scatter(summed_weight, ("row", "col"), scatter_dimension=0, tiled=True) / res_total
    )
    return (pair_output_update, alignment_gradient, projection_gradient)


def solution(mesh):
    return jax.shard_map(
        local,
        mesh=mesh,
        in_specs=(
            P("row", "col", None),
            P(),
            P(),
            P(),
            P(),
            P(),
            P(),
            P(),
            P(),
            P("row", "col", None),
        ),
        out_specs=(P("row", "col", None), P("row", "col", None), P(("row", "col"), None)),
        check_vma=False,
    )
```

profile of v0, /device:TPU:0, one launch (start us, length us, event | category | flops | bytes accessed | tf_op | source)
XLA Modules:
  0.0 286.2 jit_solution(5915464987564488654)
XLA Ops:
  7.2 1.1 reduce_sum.35
  8.4 1.1 multiply_reduce_fusion.1
  9.5 1.4 convolution_add_fusion.1
  11.0 7.2 %all_gather.7 = f32[8,64,32]{2,1,0:T(8,128)S(1)} all-gather(f32[8,32,32]{2,1,0:T(8,128)S(1)} %convolution_add_fusion.1), channel_id=1, replica_groups=mesh['row'=16,'col'=2] {'col'}, dimensions={1}, use_global_device_ids=true | all-gather | bytes 98304 | tf_op jit(solution)/shard_map/all_gather | solution.py:105
  19.1 6.1 %all-to-all-start = ((f32[16,1,1024]{2,1,0:T(1,128)}), f32[16,1,1024]{2,1,0:T(1,128)S(1)}, u32[]{:S(2)}, u32[]{:S(2)}) async-start(f32[16,1,1024]{2,1,0:T(1,128)} %reshape.63), calls=%async_computation | async-start | bytes 131072 | tf_op jit(solution)/shard_map/all_to_all | solution.py:106
  26.3 33.1 %all_gather.6 = f32[128,32,32]{2,1,0:T(8,128)} all-gather(f32[8,32,32]{2,1,0:T(8,128)S(1)} %convolution_add_fusion.2), channel_id=1, replica_groups=mesh['row'=16,'col'=2] {'row'}, dimensions={0}, use_global_device_ids=true | all-gather | bytes 557056 | tf_op jit(solution)/shard_map/all_gather | solution.py:104
  60.7 0.8 reduce
  61.6 3.4 %convolution_bitcast_fusion = f32[128,32,32]{2,0,1:T(8,128)} fusion(f32[4,32,32,32]{3,2,1,0:T(8,128)S(1)} %reshape.52, f32[8,16,4,32]{3,0,2,1:T(8,128)S(1)} %bitcast.67), kind=kOutput, calls=%fused_computation.6 | convolution fusion | flops 201326592 | bytes 1114112 | tf_op jit(solution)/shard_map/while/body/eval_jaxpr/sic,ijce->sje/dot_general | solution.py:61
  65.0 4.8 %fusion.9 = f32[128,4,32]{0,2,1:T(8,128)S(1)} fusion(f32[4,32,32,32]{3,2,1,0:T(8,128)S(1)} %reshape.52, f32[128,32,32]{2,1,0:T(8,128)} %all_gather.6), kind=kOutput, calls=%fused_computation.13 | convolution fusion | flops 201326592 | bytes 1114112 | tf_op jit(solution)/shard_map/while/body/eval_jaxpr/ijce,sje->sic/dot_general | solution.py:60
  70.0 0.8 reshape.65
  70.8 4.4 %all-to-all-start.1 = ((f32[16,1,1024]{2,1,0:T(1,128)}), f32[16,1,1024]{2,1,0:T(1,128)S(1)}, u32[]{:S(2)}, u32[]{:S(2)}) async-start(f32[16,1,1024]{2,1,0:T(1,128)} %reshape.65), calls=%async_computation.2 | async-start | bytes 131072 | tf_op jit(solution)/shard_map/all_to_all | solution.py:110
  75.4 7.8 %fusion.5 = f32[4,32,32,32]{2,3,0,1:T(8,128)} fusion(f32[128,32,32,1]{2,1,0,3:T(8,128)} %bitcast.66, f32[8,16,4,32]{3,0,2,1:T(8,128)S(1)} %bitcast.68), kind=kOutput, calls=%fused_computation.5 | convolution fusion | flops 201326592 | bytes 1114112 | tf_op jit(solution)/shard_map/while/body/eval_jaxpr/sic,sje->ijce/dot_general | solution.py:49
  83.2 1.9 copy.40
  85.2 1.0 reshape.51
  86.2 0.8 reduce.1
  87.9 1.9 fusion.12
  89.9 1.8 convolution_bitcast_fusion.1
  91.7 35.0 %reduce-scatter.4.cloned.1.call-done = f32[8,32,32]{2,0,1:T(8,128)} async-done(((f32[128,32,32]{2,0,1:T(8,128)}), f32[8,32,32]{2,0,1:T(8,128)}) %reduce-scatter.4.cloned.1.call-update) | async-done | bytes 32784 | tf_op jit(solution)/shard_map/reduce_scatter | solution.py:112
  126.7 1.3 fusion.22
  128.0 12.3 %reduce-scatter.6.cloned.1.call-done = f32[8,32,32]{2,0,1:T(8,128)} async-done(((f32[8,64,32]{2,0,1:T(8,128)}), f32[8,32,32]{2,0,1:T(8,128)}) %reduce-scatter.6.cloned.1.call-update) | async-done | bytes 32784 | tf_op jit(solution)/shard_map/reduce_scatter | solution.py:111
  140.3 1.3 multiply_reduce_fusion
  141.9 0.9 broadcast_add_fusion
  142.8 135.5 %reduce-scatter.8.cloned.1.call-done = f32[32,128]{1,0:T(8,128)} async-done(((f32[1024,128]{1,0:T(8,128)}), f32[32,128]{1,0:T(8,128)}) %reduce-scatter.8.cloned.1.call-update) | async-done | bytes 16400 | tf_op jit(solution)/shard_map/reduce_scatter | solution.py:116
  278.3 1.3 broadcast_multiply_fusion
  (42 shorter events, 5.0 us)
Async XLA Ops:
  7.2 18.6 %copy-start = (f32[1024,128]{1,0:T(8,128)S(1)}, f32[1024,128]{1,0:T(8,128)}, u32[]{:S(2)}) copy-start(f32[1024,128]{1,0:T(8,128)} %param.17) | copy-start | bytes 1572868
  7.2 18.1 %copy-start.1 = (f32[8,32,256]{2,1,0:T(8,128)S(1)}, f32[8,32,256]{2,1,0:T(8,128)}, u32[]{:S(2)}) copy-start(f32[8,32,256]{2,1,0:T(8,128)} %param.10) | copy-start | bytes 786436
  7.2 18.1 %copy-start.6 = (f32[256]{0:T(256)S(1)}, f32[256]{0:T(256)}, u32[]{:S(2)}) copy-start(f32[256]{0:T(256)} %param.11) | copy-start | bytes 3076
  7.2 18.1 %copy-start.7 = (f32[256]{0:T(256)S(1)}, f32[256]{0:T(256)}, u32[]{:S(2)}) copy-start(f32[256]{0:T(256)} %param.12) | copy-start | bytes 3076
  7.2 18.1 %copy-start.4 = (f32[256,32]{0,1:T(8,128)S(1)}, f32[256,32]{0,1:T(8,128)}, u32[]{:S(2)}) copy-start(f32[256,32]{0,1:T(8,128)} %param.15) | copy-start | bytes 98308
  7.2 18.1 %copy-start.8 = (f32[32]{0:T(128)S(1)}, f32[32]{0:T(128)}, u32[]{:S(2)}) copy-start(f32[32]{0:T(128)} %param.16) | copy-start | bytes 388
  7.2 18.5 %copy-start.2 = (f32[4,32,128]{2,1,0:T(8,128)S(1)}, f32[4,32,128]{2,1,0:T(8,128)}, u32[]{:S(2)}) copy-start(f32[4,32,128]{2,1,0:T(8,128)} %param.19) | copy-start | bytes 196612
  19.1 41.1 %all-to-all-start = ((f32[16,1,1024]{2,1,0:T(1,128)}), f32[16,1,1024]{2,1,0:T(1,128)S(1)}, u32[]{:S(2)}, u32[]{:S(2)}) async-start(f32[16,1,1024]{2,1,0:T(1,128)} %reshape.63), calls=%async_computation | async-start | bytes 131072 | tf_op jit(solution)/shard_map/all_to_all | solution.py:106
  25.2 101.5 %reduce-scatter.4.cloned.1.call-start = ((), (), s32[]{:S(2)}) async-start(), calls=%async_computation.5 | async-start | bytes 2228224 | tf_op jit(solution)/shard_map/reduce_scatter | solution.py:112
  70.8 15.4 %all-to-all-start.1 = ((f32[16,1,1024]{2,1,0:T(1,128)}), f32[16,1,1024]{2,1,0:T(1,128)S(1)}, u32[]{:S(2)}, u32[]{:S(2)}) async-start(f32[16,1,1024]{2,1,0:T(1,128)} %reshape.65), calls=%async_computation.2 | async-start | bytes 131072 | tf_op jit(solution)/shard_map/all_to_all | solution.py:110
  75.2 65.1 %reduce-scatter.6.cloned.1.call-start = ((), (), s32[]{:S(2)}) async-start(), calls=%async_computation.6 | async-start | bytes 393216 | tf_op jit(solution)/shard_map/reduce_scatter | solution.py:111
  87.1 39.6 %copy-start.5 = (f32[256,32]{0,1:T(8,128)S(1)}, f32[256,32]{0,1:T(8,128)}, u32[]{:S(2)}) copy-start(f32[256,32]{0,1:T(8,128)} %param.15) | copy-start | bytes 98308
  87.2 53.1 %copy-start.3 = (f32[256,32]{0,1:T(8,128)S(1)}, f32[256,32]{0,1:T(8,128)}, u32[]{:S(2)}) copy-start(f32[256,32]{0,1:T(8,128)} %param.13) | copy-start | bytes 98308
  89.9 188.5 %reduce-scatter.8.cloned.1.call-start = ((), (), s32[]{:S(2)}) async-start(), calls=%async_computation.7 | async-start | bytes 540672 | tf_op jit(solution)/shard_map/reduce_scatter | solution.py:116
Sparse Core Ops, SparseCore 0:
  65.1 61.5 reduce-scatter.3
  129.5 10.6 reduce-scatter.5
  142.5 135.7 reduce-scatter.7
where the time goes:
time: 287 us; the launch traced here: 286 us
  waiting for transfers between devices  183 us (64%)
  blocking collectives  40.3 us (14%)
  matrix products  24.8 us (9%)
  between operations  14 us (5%)
  starting transfers between devices  10.8 us (4%)
  local copies, waits for them, and re-layouts  7.11 us (2%)
  other arithmetic  6.36 us (2%)
    reduce_scatter x1, waiting for transfers between devices, local(): lax.psum_scatter(summed_weight, ('row', 'col'), scatter_dimension=0, tile...  136 us
    reduce_scatter x1, waiting for transfers between devices, local(): lax.psum_scatter(right_sum, 'row', scatter_dimension=0, tiled=True)  35 us
    all_gather x1, blocking collectives, local(): lax.all_gather(second_operand_portion, 'row', axis=0, tiled=True)  33.1 us
    reduce_scatter x1, waiting for transfers between devices, local(): lax.psum_scatter(swapped, 'col', scatter_dimension=1, tiled=True)  12.3 us
    dot_general x1, matrix products, tile_step(): jnp.einsum('sic,sje->ijce', left_blk, right_all, precision=precise)  7.84 us
    all_gather x1, blocking collectives, local(): widened = lax.all_gather(first_operand_portion, 'col', axis=1, tiled=True)  7.15 us
    all_to_all x1, starting transfers between devices, local(): lax.all_to_all(widened, 'row', split_axis=1, concat_axis=0, tiled=True)  6.13 us
  transfers between devices with their start and end apart: 5, of which 3 were waited for; matrix products, arithmetic and copies ran while one was open for 10% of the time, Pallas kernels for 0%

commit v1 on v0

v1 whole, which is shorter than its diff:
```python
import functools

import jax
import jax.numpy as jnp
from jax import lax
from jax.experimental import pallas as pl
from jax.experimental.pallas import tpu as pltpu
from jax.sharding import PartitionSpec as P

MESH = pl.DeviceIdType.MESH
LANES = 128

NN = (((1,), (0,)), ((), ()))
NT = (((1,), (1,)), ((), ()))
TN = (((0,), (0,)), ((), ()))


def split(a):
    hi = a.astype(jnp.bfloat16)
    return hi, (a - hi.astype(jnp.float32)).astype(jnp.bfloat16)


def mul(a, b, dims):
    (ah, al), (bh, bl) = a, b
    one = functools.partial(lax.dot_general, dimension_numbers=dims, preferred_element_type=jnp.float32)
    return one(ah, bh) + (one(ah, bl) + one(al, bh))


def block_transpose(parts, width):
    parts = list(parts)
    count = len(parts)
    block = lax.broadcasted_iota(jnp.int32, parts[0].shape, 1) // width
    half = count // 2
    while half >= 1:
        low = (block & half) == 0
        for a in range(count):
            if a & half:
                continue
            va, vb = parts[a], parts[a + half]
            parts[a] = jnp.where(low, va, pltpu.roll(vb, half * width, 1))
            parts[a + half] = jnp.where(low, pltpu.roll(va, LANES - half * width, 1), vb)
        half //= 2
    return parts


def kernel(
    n_row, n_col, s_loc, tile_i, tile_j, chans,
    x_ref, scale_ref, offset_ref, w1_ref, b1_ref, w2_ref, b2_ref, wr_ref, br_ref, cot_ref,
    pair_ref, ag_ref, proj_ref,
    xs, xhat, rstd, mixl, mixr, wt, rsend, lsend, r_all, l_all, wp, mt, gt, outer, pp, psend, precv,
    rgrad, lgrad, rrecv, lrecv, send_sems, recv_sems, bar_sems,
):
    row, col = lax.axis_index("row"), lax.axis_index("col")
    n_dev = n_row * n_col
    me = row * n_col + col
    rows_all = n_row * s_loc
    feats = x_ref.shape[1]
    q = LANES // chans
    groups = tile_j // q
    per_col = tile_j // tile_i
    owner = row // per_col
    place = row % per_col
    rp = proj_ref.shape[0]

    barrier = pltpu.get_barrier_semaphore()

    @pl.loop(1, n_dev)
    def _(d):
        t = lax.rem(me + d, n_dev)
        pl.semaphore_signal(barrier, inc=1, device_id=(t // n_col, lax.rem(t, n_col)), device_id_type=MESH)

    lane_block = lax.broadcasted_iota(jnp.int32, (feats, LANES), 1) // chans
    w1t = jnp.concatenate([w1_ref[...]] * q, axis=1)
    w2t = jnp.concatenate([w2_ref[...]] * q, axis=1)
    accl = jnp.concatenate([b1_ref[...]] * q, axis=1)
    accr = jnp.concatenate([b2_ref[...]] * q, axis=1)
    acc = jnp.concatenate([accl, accr], axis=1)
    for h in range(feats // LANES):
        xs[h] = x_ref[:, h * LANES : (h + 1) * LANES]
    for k in range(q):
        wk = jnp.concatenate(
            [jnp.where(lane_block == k, w1t, 0.0), jnp.where(lane_block == k, w2t, 0.0)], axis=1
        )
        wt[k] = wk
        halves = [
            xs[h, pl.ds(k, s_loc * groups, stride=q), :] for h in range(feats // LANES)
        ]
        xk = jnp.concatenate(halves, axis=1)
        dk = xk - jnp.mean(xk, axis=1, keepdims=True)
        rk = lax.rsqrt(jnp.mean(dk * dk, axis=1, keepdims=True) + 1e-05)
        hat = dk * rk
        xhat[k] = hat
        rstd[k] = rk
        acc = acc + mul(split(hat * scale_ref[...] + offset_ref[...]), split(wk), NN)
    mixl[...] = acc[:, :LANES]
    mixr[...] = acc[:, LANES:]
    for g in range(groups):
        rsend[:, g * LANES : (g + 1) * LANES] = mixr[pl.ds(g, s_loc, stride=groups), :]
        b, off = (g * q) // tile_i, (g * q) % tile_i * chans
        lsend[b, :, off : off + LANES] = mixl[pl.ds(g, s_loc, stride=groups), :]

    pl.semaphore_wait(barrier, n_dev - 1)

    @pl.loop(1, n_row)
    def _(d):
        t = lax.rem(row + d, n_row)
        pltpu.make_async_remote_copy(
            src_ref=rsend, dst_ref=r_all.at[row], send_sem=send_sems.at[0], recv_sem=recv_sems.at[0],
            device_id=(t, col), device_id_type=MESH,
        ).start()

    def send_left(b, c):
        pltpu.make_async_remote_copy(
            src_ref=lsend.at[b], dst_ref=l_all.at[row], send_sem=send_sems.at[1], recv_sem=recv_sems.at[1],
            device_id=(col * per_col + b, c), device_id_type=MESH,
        ).start()

    mine = owner == col

    @pl.loop(0, per_col)
    def _(b):
        @pl.loop(0, n_col)
        def _(c):
            other = jnp.logical_or(c != col, col * per_col + b != row)

            @pl.when(other)
            def _():
                send_left(b, c)

    r_all[row] = rsend[...]

    @pl.when(mine)
    def _():
        l_all[row] = lsend[place]

    for e in range(chans):
        wp[pl.ds(e * chans, chans), :] = wr_ref[pl.ds(e, chans, stride=chans), :]
    cots = split(cot_ref[...])
    wps = split(wp[...])
    outer[...] = mul(cots, wps, NT) * (1.0 / rows_all)
    for ig in range(tile_i // q):
        for eg in range(chans // q):
            parts = [
                outer[(ig * q + k) * tile_j : (ig * q + k + 1) * tile_j, eg * LANES : (eg + 1) * LANES]
                for k in range(q)
            ]
            for k, part in enumerate(block_transpose(parts, chans)):
                gt[ig, pl.ds(eg * q + k, tile_j, stride=chans), :] = part
    gts = split(jnp.concatenate([gt[ig] for ig in range(tile_i // q)], axis=1))

    def wait(ref, sem):
        pltpu.make_async_copy(ref, ref, sem).wait()

    wait(r_all.at[pl.ds(0, n_row - 1)], recv_sems.at[0])

    @pl.when(mine)
    def _():
        wait(l_all.at[pl.ds(0, n_row - 1)], recv_sems.at[1])

    @pl.when(jnp.logical_not(mine))
    def _():
        wait(l_all, recv_sems.at[1])

    right = split(r_all[...].reshape(rows_all, tile_j * chans))
    left = split(l_all[...].reshape(rows_all, tile_i * chans))
    product = mul(right, left, TN)
    for ig in range(tile_i // q):
        mt[ig] = product[:, ig * LANES : (ig + 1) * LANES]
    for ig in range(tile_i // q):
        for eg in range(chans // q):
            parts = [
                mt[ig, pl.ds(eg * q + k, tile_j, stride=chans), :] for k in range(q)
            ]
            for k, part in enumerate(block_transpose(parts, chans)):
                outer[(ig * q + k) * tile_j : (ig * q + k + 1) * tile_j, eg * LANES : (eg + 1) * LANES] = part
    outers = split(outer[...])
    pp[...] = mul(outers, cots, TN)
    per = chans // rp
    for c in range(chans):
        rows = pp[pl.ds(c, chans, stride=chans), :]
        for t in range(per):
            psend[c * per + t] = rows[t * rp : (t + 1) * rp]

    @pl.loop(1, n_dev)
    def _(d):
        t = lax.rem(me + d, n_dev)
        pltpu.make_async_remote_copy(
            src_ref=psend.at[t], dst_ref=precv.at[me], send_sem=send_sems.at[2], recv_sem=recv_sems.at[2],
            device_id=(t // n_col, lax.rem(t, n_col)), device_id_type=MESH,
        ).start()

    rgrad[...] = mul(left, gts, NT).reshape(n_row, s_loc, tile_j * chans)

    @pl.loop(1, n_row)
    def _(d):
        t = lax.rem(row + d, n_row)
        pltpu.make_async_remote_copy(
            src_ref=rgrad.at[t], dst_ref=rrecv.at[row], send_sem=send_sems.at[3], recv_sem=recv_sems.at[3],
            device_id=(t, col), device_id_type=MESH,
        ).start()

    lgrad[...] = mul(right, gts, NN).reshape(n_row, s_loc, tile_i * chans)

    @pl.loop(0, n_row)
    def _(t):
        @pl.when(jnp.logical_or(t != row, owner != col))
        def _():
            pltpu.make_async_remote_copy(
                src_ref=lgrad.at[t], dst_ref=lrecv.at[col * per_col + place],
                send_sem=send_sems.at[4], recv_sem=recv_sems.at[4],
                device_id=(t, owner), device_id_type=MESH,
            ).start()

    pair_ref[...] = mul(outers, wps, NN) * (1.0 / rows_all) + br_ref[...]

    precv[me] = psend[me]
    rrecv[row] = rgrad[row]

    @pl.when(mine)
    def _():
        lrecv[col * per_col + place] = lgrad[row]

    wait(rrecv.at[pl.ds(0, n_row - 1)], recv_sems.at[3])

    @pl.when(mine)
    def _():
        wait(lrecv.at[pl.ds(0, n_row - 1)], recv_sems.at[4])

    @pl.when(jnp.logical_not(mine))
    def _():
        wait(lrecv, recv_sems.at[4])

    rsum = jnp.sum(rrecv[...], axis=0)
    lsum = lrecv[pl.ds(0, per_col)]
    for c in range(1, n_col):
        lsum = lsum + lrecv[pl.ds(c * per_col, per_col)]
    for g in range(groups):
        b, off = (g * q) // tile_i, (g * q) % tile_i * chans
        mixr[pl.ds(g, s_loc, stride=groups), :] = rsum[:, g * LANES : (g + 1) * LANES]
        mixl[pl.ds(g, s_loc, stride=groups), :] = lsum[b, :, off : off + LANES]
    grads = split(jnp.concatenate([mixl[...], mixr[...]], axis=1))
    for k in range(q):
        dk = mul(grads, split(wt[k]), NT) * scale_ref[...]
        hat = xhat[k]
        back = rstd[k] * (
            dk - jnp.mean(dk, axis=1, keepdims=True) - hat * jnp.mean(dk * hat, axis=1, keepdims=True)
        )
        for h in range(feats // LANES):
            xs[h, pl.ds(k, s_loc * groups, stride=q), :] = back[:, h * LANES : (h + 1) * LANES]
    for h in range(feats // LANES):
        ag_ref[:, h * LANES : (h + 1) * LANES] = xs[h]

    wait(precv.at[pl.ds(0, n_dev - 1)], recv_sems.at[2])
    proj_ref[...] = jnp.sum(precv[...], axis=0) * (1.0 / (tile_j * n_col))

    wait(r_all.at[pl.ds(0, n_row - 1)], send_sems.at[0])

    @pl.when(mine)
    def _():
        wait(l_all.at[pl.ds(0, per_col * n_col - 1)], send_sems.at[1])
        wait(lrecv.at[pl.ds(0, n_row - 1)], send_sems.at[4])

    @pl.when(jnp.logical_not(mine))
    def _():
        wait(l_all, send_sems.at[1])
        wait(lrecv, send_sems.at[4])

    wait(precv.at[pl.ds(0, n_dev - 1)], send_sems.at[2])
    wait(rrecv.at[pl.ds(0, n_row - 1)], send_sems.at[3])


def solution(mesh):
    n_row, n_col = mesh.shape["row"], mesh.shape["col"]
    n_dev = n_row * n_col

    def local(x, scale, offset, w1, b1, w2, b2, wr, br, cot):
        s_loc, tile_j, feats = x.shape
        tile_i, _, pair_ch = cot.shape
        chans = w1.shape[1]
        rows_all = n_row * s_loc
        q = LANES // chans
        groups = tile_j // q
        per_col = tile_j // tile_i
        rp = chans * chans // n_dev
        f32 = jnp.float32
        vm = lambda *shape: pltpu.VMEM(shape, f32)
        wide, thin = tile_j * chans, tile_i * chans
        pair, grad, proj = pl.pallas_call(
            functools.partial(kernel, n_row, n_col, s_loc, tile_i, tile_j, chans),
            out_shape=(
                jax.ShapeDtypeStruct((tile_i * tile_j, pair_ch), f32),
                jax.ShapeDtypeStruct((s_loc * tile_j, feats), f32),
                jax.ShapeDtypeStruct((rp, pair_ch), f32),
            ),
            in_specs=[pl.BlockSpec(memory_space=pltpu.VMEM)] * 10,
            out_specs=(pl.BlockSpec(memory_space=pltpu.VMEM),) * 3,
            scratch_shapes=[
                vm(feats // LANES, s_loc * tile_j, LANES),
                vm(q, s_loc * groups, feats),
                vm(q, s_loc * groups, 1),
                vm(s_loc * groups, LANES),
                vm(s_loc * groups, LANES),
                vm(q, feats, 2 * LANES),
                vm(s_loc, wide),
                vm(per_col, s_loc, thin),
                vm(n_row, s_loc, wide),
                vm(n_row, s_loc, thin),
                vm(chans * chans, pair_ch),
                vm(tile_i // q, wide, LANES),
                vm(tile_i // q, wide, LANES),
                vm(tile_i * tile_j, chans * chans),
                vm(chans * chans, pair_ch),
                vm(n_dev, rp, pair_ch),
                vm(n_dev, rp, pair_ch),
                vm(n_row, s_loc, wide),
                vm(n_row, s_loc, thin),
                vm(n_row, s_loc, wide),
                vm(n_col * per_col, s_loc, thin),
                pltpu.SemaphoreType.DMA((5,)),
                pltpu.SemaphoreType.DMA((5,)),
                pltpu.SemaphoreType.DMA((1,)),
            ],
            compiler_params=pltpu.CompilerParams(
                collective_id=0, has_side_effects=True, vmem_limit_bytes=60 * 1024 * 1024
            ),
        )(
            x.reshape(s_loc * tile_j, feats), scale.reshape(1, -1), offset.reshape(1, -1),
            w1, b1.reshape(1, -1), w2, b2.reshape(1, -1), wr, br.reshape(1, -1),
            cot.reshape(tile_i * tile_j, pair_ch),
        )
        return (
            pair.reshape(tile_i, tile_j, pair_ch),
            grad.reshape(s_loc, tile_j, feats),
            proj,
        )

    return jax.shard_map(
        local,
        mesh=mesh,
        in_specs=(
            P("row", "col", None), P(), P(), P(), P(), P(), P(), P(), P(), P("row", "col", None),
        ),
        out_specs=(P("row", "col", None), P("row", "col", None), P(("row", "col"), None)),
        check_vma=False,
    )
```

time: 287 us -> 59.7 us (0.21)
  the two profiles are of different devices: /device:TPU:0 before, /device:TPU:24 now
where the time goes in v1:
time: 59.7 us; the launch traced here: 58.5 us
  Pallas kernels  51.8 us (87%)
  local copies, waits for them, and re-layouts  6.06 us (10%)
  between operations  0.65 us (1%)
    pallas_call x1, Pallas kernels, local(): pl.pallas_call(functools.partial(kernel, n_row, n_col, s_loc, tile_i, til...  51.8 us
    unnamed x9, local copies, waits for them, and re-layouts  6.06 us

profile of v1, /device:TPU:24, one launch (start us, length us, event | category | flops | bytes accessed | tf_op | source)
XLA Modules:
  0.0 58.5 jit_solution(10046582121179167798)
XLA Ops:
  0.6 0.0 copy-start
  0.6 1.5 %copy.13.w1_ref = f32[256,32]{1,0:T(8,128)} copy(f32[256,32]{0,1:T(8,128)} %param.13) | data formatting | bytes 65536 | tf_op args[3]
  2.2 0.0 copy-done
  2.2 0.8 %copy.14.w2_ref = f32[256,32]{1,0:T(8,128)} copy(f32[256,32]{0,1:T(8,128)S(1)} %copy-done) | data formatting | bytes 65536 | tf_op args[5]
  2.9 51.8 %shard_map.121 = (f32[128,128]{1,0:T(8,128)}, f32[256,256]{1,0:T(8,128)}, f32[32,128]{1,0:T(8,128)}) custom-call(f32[256,256]{1,0:T(8,128)} %bitcast.9, f32[1,256]{1,0:T(1,128)} %bitcast.13, f32[1,256]{1,0:T(1,128)} %bitcast.14, f32[256,32]{1,0:T(8,128)} %copy.13.w1_ref, f32[1,32]{1,0:T(1,128)} %bitcast.15, f32[256,32]{1,0:T(8,128)} %copy.14.w2_ref, ...), custom_call_target="tpu_custom_call" | custom-call | tf_op jit(solution)/shard_map/pallas_call | solution.py:288
  54.8 1.5 %copy.18 = f32[4,32,128]{2,1,0:T(8,128)} copy(f32[4,32,128]{2,1,0:T(8,128)} %bitcast.12) | data formatting | bytes 131072
  56.3 0.0 copy-start.1
  56.3 1.7 %copy.19 = f32[8,32,256]{2,1,0:T(8,128)} copy(f32[8,32,256]{2,1,0:T(8,128)} %bitcast.10) | data formatting | bytes 524288
  57.9 0.0 copy-done.1
  57.9 0.6 %copy.20 = f32[32,128]{1,0:T(8,128)} copy(f32[32,128]{1,0:T(8,128)S(1)} %copy-done.1) | data formatting | bytes 32768
Async XLA Ops:
  0.6 1.5 %copy-start = (f32[256,32]{0,1:T(8,128)S(1)}, f32[256,32]{0,1:T(8,128)}, u32[]{:S(2)}) copy-start(f32[256,32]{0,1:T(8,128)} %param.15) | copy-start | bytes 98308
  56.3 1.7 %copy-start.1 = (f32[32,128]{1,0:T(8,128)S(1)}, f32[32,128]{1,0:T(8,128)}, u32[]{:S(2)}) copy-start(f32[32,128]{1,0:T(8,128)} %get-tuple-element.14) | copy-start | bytes 49156

commit v2 on v1

--- a/solution.py
+++ b/solution.py
@@ -47,8 +47,8 @@
     n_row, n_col, s_loc, tile_i, tile_j, chans,
     x_ref, scale_ref, offset_ref, w1_ref, b1_ref, w2_ref, b2_ref, wr_ref, br_ref, cot_ref,
     pair_ref, ag_ref, proj_ref,
-    xs, xhat, rstd, mixl, mixr, wt, rsend, lsend, r_all, l_all, wp, mt, gt, outer, pp, psend, precv,
-    rgrad, lgrad, rrecv, lrecv, send_sems, recv_sems, bar_sems,
+    xs, xhat, rstd, mixl, mixr, wt, rsend, lsend, r_all, l_all, wp, mt, gt, outer, pp, psend, pmid, pout, precv,
+    rgrad, rmid, rout, lgrad, rrecv, lrecv, send_sems, recv_sems,
 ):
     row, col = lax.axis_index("row"), lax.axis_index("col")
     n_dev = n_row * n_col
@@ -61,6 +61,11 @@
     owner = row // per_col
     place = row % per_col
     rp = proj_ref.shape[0]
+    core, chip, n_chip = row % 2, row // 2, n_row // 2
+    slot = core * n_chip + chip
+    partner = (row + 1 - 2 * core, col)
+    half = n_chip * n_col
+    spot = chip * n_col + col
 
     barrier = pltpu.get_barrier_semaphore()
 
@@ -69,18 +74,16 @@
         t = lax.rem(me + d, n_dev)
         pl.semaphore_signal(barrier, inc=1, device_id=(t // n_col, lax.rem(t, n_col)), device_id_type=MESH)
 
-    lane_block = lax.broadcasted_iota(jnp.int32, (feats, LANES), 1) // chans
-    w1t = jnp.concatenate([w1_ref[...]] * q, axis=1)
-    w2t = jnp.concatenate([w2_ref[...]] * q, axis=1)
     accl = jnp.concatenate([b1_ref[...]] * q, axis=1)
     accr = jnp.concatenate([b2_ref[...]] * q, axis=1)
     acc = jnp.concatenate([accl, accr], axis=1)
     for h in range(feats // LANES):
         xs[h] = x_ref[:, h * LANES : (h + 1) * LANES]
     for k in range(q):
-        wk = jnp.concatenate(
-            [jnp.where(lane_block == k, w1t, 0.0), jnp.where(lane_block == k, w2t, 0.0)], axis=1
-        )
+        blank = jnp.zeros((chans, feats), jnp.float32)
+        pieces = [blank] * (2 * q)
+        pieces[k], pieces[q + k] = w1_ref[...], w2_ref[...]
+        wk = jnp.concatenate(pieces, axis=0)
         wt[k] = wk
         halves = [
             xs[h, pl.ds(k, s_loc * groups, stride=q), :] for h in range(feats // LANES)
@@ -91,7 +94,7 @@
         hat = dk * rk
         xhat[k] = hat
         rstd[k] = rk
-        acc = acc + mul(split(hat * scale_ref[...] + offset_ref[...]), split(wk), NN)
+        acc = acc + mul(split(hat * scale_ref[...] + offset_ref[...]), split(wk), NT)
     mixl[...] = acc[:, :LANES]
     mixr[...] = acc[:, LANES:]
     for g in range(groups):
@@ -101,17 +104,9 @@
 
     pl.semaphore_wait(barrier, n_dev - 1)
 
-    @pl.loop(1, n_row)
-    def _(d):
-        t = lax.rem(row + d, n_row)
-        pltpu.make_async_remote_copy(
-            src_ref=rsend, dst_ref=r_all.at[row], send_sem=send_sems.at[0], recv_sem=recv_sems.at[0],
-            device_id=(t, col), device_id_type=MESH,
-        ).start()
-
     def send_left(b, c):
         pltpu.make_async_remote_copy(
-            src_ref=lsend.at[b], dst_ref=l_all.at[row], send_sem=send_sems.at[1], recv_sem=recv_sems.at[1],
+            src_ref=lsend.at[b], dst_ref=l_all.at[slot], send_sem=send_sems.at[1], recv_sem=recv_sems.at[1],
             device_id=(col * per_col + b, c), device_id_type=MESH,
         ).start()
 
@@ -127,11 +122,19 @@
             def _():
                 send_left(b, c)
 
-    r_all[row] = rsend[...]
-
-    @pl.when(mine)
-    def _():
-        l_all[row] = lsend[place]
+    @pl.loop(1, n_chip)
+    def _(d):
+        t = lax.rem(chip + d, n_chip)
+        pltpu.make_async_remote_copy(
+            src_ref=rsend, dst_ref=r_all.at[slot], send_sem=send_sems.at[0], recv_sem=recv_sems.at[0],
+            device_id=(t * 2 + core, col), device_id_type=MESH,
+        ).start()
+
+    r_all[slot] = rsend[...]
+
+    @pl.when(mine)
+    def _():
+        l_all[slot] = lsend[place]
 
     for e in range(chans):
         wp[pl.ds(e * chans, chans), :] = wr_ref[pl.ds(e, chans, stride=chans), :]
@@ -151,8 +154,6 @@
     def wait(ref, sem):
         pltpu.make_async_copy(ref, ref, sem).wait()
 
-    wait(r_all.at[pl.ds(0, n_row - 1)], recv_sems.at[0])
-
     @pl.when(mine)
     def _():
         wait(l_all.at[pl.ds(0, n_row - 1)], recv_sems.at[1])
@@ -161,8 +162,34 @@
     def _():
         wait(l_all, recv_sems.at[1])
 
+    left = split(l_all[...].reshape(rows_all, tile_i * chans))
+    rgrad[...] = mul(left, gts, NT).reshape(n_row, s_loc, tile_j * chans)
+
+    def to_partner(src, dst, at):
+        pltpu.make_async_remote_copy(
+            src_ref=src, dst_ref=dst, send_sem=send_sems.at[at], recv_sem=recv_sems.at[at],
+            device_id=partner, device_id_type=MESH,
+        ).start()
+
+    to_partner(rgrad.at[pl.ds((1 - core) * n_chip, n_chip)], rmid, 5)
+    wait(rmid, recv_sems.at[5])
+    rout[...] = rgrad[pl.ds(core * n_chip, n_chip)] + rmid[...]
+
+    @pl.loop(1, n_chip)
+    def _(d):
+        t = lax.rem(chip + d, n_chip)
+        pltpu.make_async_remote_copy(
+            src_ref=rout.at[t], dst_ref=rrecv.at[chip], send_sem=send_sems.at[3], recv_sem=recv_sems.at[3],
+            device_id=(t * 2 + core, col), device_id_type=MESH,
+        ).start()
+
+    rrecv[chip] = rout[chip]
+
+    wait(r_all.at[pl.ds(0, n_chip - 1)], recv_sems.at[0])
+    shared = r_all.at[pl.ds(core * n_chip, n_chip)]
+    to_partner(shared, shared, 6)
+    wait(r_all.at[pl.ds(0, n_chip)], recv_sems.at[6])
     right = split(r_all[...].reshape(rows_all, tile_j * chans))
-    left = split(l_all[...].reshape(rows_all, tile_i * chans))
     product = mul(right, left, TN)
     for ig in range(tile_i // q):
         mt[ig] = product[:, ig * LANES : (ig + 1) * LANES]
@@ -179,26 +206,11 @@
     for c in range(chans):
         rows = pp[pl.ds(c, chans, stride=chans), :]
         for t in range(per):
-            psend[c * per + t] = rows[t * rp : (t + 1) * rp]
-
-    @pl.loop(1, n_dev)
-    def _(d):
-        t = lax.rem(me + d, n_dev)
-        pltpu.make_async_remote_copy(
-            src_ref=psend.at[t], dst_ref=precv.at[me], send_sem=send_sems.at[2], recv_sem=recv_sems.at[2],
-            device_id=(t // n_col, lax.rem(t, n_col)), device_id_type=MESH,
-        ).start()
-
-    rgrad[...] = mul(left, gts, NT).reshape(n_row, s_loc, tile_j * chans)
-
-    @pl.loop(1, n_row)
-    def _(d):
-        t = lax.rem(row + d, n_row)
-        pltpu.make_async_remote_copy(
-            src_ref=rgrad.at[t], dst_ref=rrecv.at[row], send_sem=send_sems.at[3], recv_sem=recv_sems.at[3],
-            device_id=(t, col), device_id_type=MESH,
-        ).start()
-
+            p = c * per + t
+            place_of = p // n_col % 2 * half + p // n_col // 2 * n_col + p % n_col
+            psend[place_of] = rows[t * rp : (t + 1) * rp]
+
+    to_partner(psend.at[pl.ds((1 - core) * half, half)], pmid, 7)
     lgrad[...] = mul(right, gts, NN).reshape(n_row, s_loc, tile_i * chans)
 
     @pl.loop(0, n_row)
@@ -206,21 +218,31 @@
         @pl.when(jnp.logical_or(t != row, owner != col))
         def _():
             pltpu.make_async_remote_copy(
-                src_ref=lgrad.at[t], dst_ref=lrecv.at[col * per_col + place],
+                src_ref=lgrad.at[(t % 2) * n_chip + t // 2], dst_ref=lrecv.at[col * per_col + place],
                 send_sem=send_sems.at[4], recv_sem=recv_sems.at[4],
                 device_id=(t, owner), device_id_type=MESH,
             ).start()
 
+    wait(pmid, recv_sems.at[7])
+    pout[...] = psend[pl.ds(core * half, half)] + pmid[...]
+
+    @pl.loop(1, half)
+    def _(d):
+        t = lax.rem(spot + d, half)
+        pltpu.make_async_remote_copy(
+            src_ref=pout.at[t], dst_ref=precv.at[spot], send_sem=send_sems.at[2], recv_sem=recv_sems.at[2],
+            device_id=(t // n_col * 2 + core, lax.rem(t, n_col)), device_id_type=MESH,
+        ).start()
+
     pair_ref[...] = mul(outers, wps, NN) * (1.0 / rows_all) + br_ref[...]
 
-    precv[me] = psend[me]
-    rrecv[row] = rgrad[row]
-
-    @pl.when(mine)
-    def _():
-        lrecv[col * per_col + place] = lgrad[row]
-
-    wait(rrecv.at[pl.ds(0, n_row - 1)], recv_sems.at[3])
+    precv[spot] = pout[spot]
+
+    @pl.when(mine)
+    def _():
+        lrecv[col * per_col + place] = lgrad[slot]
+
+    wait(rrecv.at[pl.ds(0, n_chip - 1)], recv_sems.at[3])
 
     @pl.when(mine)
     def _():
@@ -240,7 +262,7 @@
         mixl[pl.ds(g, s_loc, stride=groups), :] = lsum[b, :, off : off + LANES]
     grads = split(jnp.concatenate([mixl[...], mixr[...]], axis=1))
     for k in range(q):
-        dk = mul(grads, split(wt[k]), NT) * scale_ref[...]
+        dk = mul(grads, split(wt[k]), NN) * scale_ref[...]
         hat = xhat[k]
         back = rstd[k] * (
             dk - jnp.mean(dk, axis=1, keepdims=True) - hat * jnp.mean(dk * hat, axis=1, keepdims=True)
@@ -250,10 +272,13 @@
     for h in range(feats // LANES):
         ag_ref[:, h * LANES : (h + 1) * LANES] = xs[h]
 
-    wait(precv.at[pl.ds(0, n_dev - 1)], recv_sems.at[2])
+    wait(precv.at[pl.ds(0, half - 1)], recv_sems.at[2])
     proj_ref[...] = jnp.sum(precv[...], axis=0) * (1.0 / (tile_j * n_col))
 
-    wait(r_all.at[pl.ds(0, n_row - 1)], send_sems.at[0])
+    wait(r_all.at[pl.ds(0, n_chip - 1)], send_sems.at[0])
+    wait(rmid, send_sems.at[5])
+    wait(shared, send_sems.at[6])
+    wait(pmid, send_sems.at[7])
 
     @pl.when(mine)
     def _():
@@ -265,8 +290,8 @@
         wait(l_all, send_sems.at[1])
         wait(lrecv, send_sems.at[4])
 
-    wait(precv.at[pl.ds(0, n_dev - 1)], send_sems.at[2])
-    wait(rrecv.at[pl.ds(0, n_row - 1)], send_sems.at[3])
+    wait(precv.at[pl.ds(0, half - 1)], send_sems.at[2])
+    wait(rrecv.at[pl.ds(0, n_chip - 1)], send_sems.at[3])
 
 
 def solution(mesh):
@@ -300,7 +325,7 @@
                 vm(q, s_loc * groups, 1),
                 vm(s_loc * groups, LANES),
                 vm(s_loc * groups, LANES),
-                vm(q, feats, 2 * LANES),
+                vm(q, 2 * LANES, feats),
                 vm(s_loc, wide),
                 vm(per_col, s_loc, thin),
                 vm(n_row, s_loc, wide),
@@ -311,21 +336,24 @@
                 vm(tile_i * tile_j, chans * chans),
                 vm(chans * chans, pair_ch),
                 vm(n_dev, rp, pair_ch),
-                vm(n_dev, rp, pair_ch),
+                vm(n_dev // 2, rp, pair_ch),
+                vm(n_dev // 2, rp, pair_ch),
+                vm(n_dev // 2, rp, pair_ch),
                 vm(n_row, s_loc, wide),
+                vm(n_row // 2, s_loc, wide),
+                vm(n_row // 2, s_loc, wide),
                 vm(n_row, s_loc, thin),
-                vm(n_row, s_loc, wide),
+                vm(n_row // 2, s_loc, wide),
                 vm(n_col * per_col, s_loc, thin),
-                pltpu.SemaphoreType.DMA((5,)),
-                pltpu.SemaphoreType.DMA((5,)),
-                pltpu.SemaphoreType.DMA((1,)),
+                pltpu.SemaphoreType.DMA((8,)),
+                pltpu.SemaphoreType.DMA((8,)),
             ],
             compiler_params=pltpu.CompilerParams(
                 collective_id=0, has_side_effects=True, vmem_limit_bytes=60 * 1024 * 1024
             ),
         )(
             x.reshape(s_loc * tile_j, feats), scale.reshape(1, -1), offset.reshape(1, -1),
-            w1, b1.reshape(1, -1), w2, b2.reshape(1, -1), wr, br.reshape(1, -1),
+            w1.T, b1.reshape(1, -1), w2.T, b2.reshape(1, -1), wr, br.reshape(1, -1),
             cot.reshape(tile_i * tile_j, pair_ch),
         )
         return (

time: 59.7 us -> 35.7 us (0.60); the launches traced: 58.5 us -> 35.5 us
  Pallas kernels: 51.8 us -> 31.1 us
  local copies, waits for them, and re-layouts: 6.06 us -> 3.77 us
    pallas_call x1, Pallas kernels: 51.8 us -> 31.1 us  [local(): pl.pallas_call(functools.partial(kernel, n_row, n_col, s_loc, tile_i, til...]
    unnamed x9 -> x5, local copies, waits for them, and re-layouts: 6.06 us -> 3.77 us
where the time goes in v2:
time: 35.7 us; the launch traced here: 35.5 us
  Pallas kernels  31.1 us (87%)
  local copies, waits for them, and re-layouts  3.77 us (11%)
  between operations  0.64 us (2%)
    pallas_call x1, Pallas kernels, local(): pl.pallas_call(functools.partial(kernel, n_row, n_col, s_loc, tile_i, til...  31.1 us
    unnamed x5, local copies, waits for them, and re-layouts  3.77 us

profile of v2, /device:TPU:24, one launch (start us, length us, event | category | flops | bytes accessed | tf_op | source)
XLA Modules:
  0.0 35.5 jit_solution(1815250137437889615)
XLA Ops:
  0.6 31.1 %shard_map.121 = (f32[128,128]{1,0:T(8,128)}, f32[256,256]{1,0:T(8,128)}, f32[32,128]{1,0:T(8,128)}) custom-call(f32[256,256]{1,0:T(8,128)} %bitcast.12, f32[1,256]{1,0:T(1,128)} %bitcast.17, f32[1,256]{1,0:T(1,128)} %bitcast.18, f32[32,256]{1,0:T(8,128)} %bitcast.15, f32[1,32]{1,0:T(1,128)} %bitcast.19, f32[32,256]{1,0:T(8,128)} %bitcast.16, ...), custom_call_target="tpu_custom_call" | custom-call | tf_op jit(solution)/shard_map/pallas_call | solution.py:313
  31.8 1.5 %copy.16 = f32[4,32,128]{2,1,0:T(8,128)} copy(f32[4,32,128]{2,1,0:T(8,128)} %bitcast.13) | data formatting | bytes 131072
  33.2 0.0 copy-start
  33.2 1.7 %copy.17 = f32[8,32,256]{2,1,0:T(8,128)} copy(f32[8,32,256]{2,1,0:T(8,128)} %bitcast.11) | data formatting | bytes 524288
  34.9 0.0 copy-done
  34.9 0.6 %copy.18 = f32[32,128]{1,0:T(8,128)} copy(f32[32,128]{1,0:T(8,128)S(1)} %copy-done) | data formatting | bytes 32768
Async XLA Ops:
  33.2 1.7 %copy-start = (f32[32,128]{1,0:T(8,128)S(1)}, f32[32,128]{1,0:T(8,128)}, u32[]{:S(2)}) copy-start(f32[32,128]{1,0:T(8,128)} %get-tuple-element.14) | copy-start | bytes 49156

commit v3 on v2

--- a/solution.py
+++ b/solution.py
@@ -45,7 +45,7 @@
 
 def kernel(
     n_row, n_col, s_loc, tile_i, tile_j, chans,
-    x_ref, scale_ref, offset_ref, w1_ref, b1_ref, w2_ref, b2_ref, wr_ref, br_ref, cot_ref,
+    x_ref, scale_ref, offset_ref, w1_ref, b1_ref, w2_ref, b2_ref, wr_ref, cot_ref,
     pair_ref, ag_ref, proj_ref,
     xs, xhat, rstd, mixl, mixr, wt, rsend, lsend, r_all, l_all, wp, mt, gt, outer, pp, psend, pmid, pout, precv,
     rgrad, rmid, rout, lgrad, rrecv, lrecv, send_sems, recv_sems,
@@ -234,7 +234,7 @@
             device_id=(t // n_col * 2 + core, lax.rem(t, n_col)), device_id_type=MESH,
         ).start()
 
-    pair_ref[...] = mul(outers, wps, NN) * (1.0 / rows_all) + br_ref[...]
+    pair_ref[...] = mul(outers, wps, NN)
 
     precv[spot] = pout[spot]
 
@@ -273,7 +273,7 @@
         ag_ref[:, h * LANES : (h + 1) * LANES] = xs[h]
 
     wait(precv.at[pl.ds(0, half - 1)], recv_sems.at[2])
-    proj_ref[...] = jnp.sum(precv[...], axis=0) * (1.0 / (tile_j * n_col))
+    proj_ref[...] = jnp.sum(precv[...], axis=0)
 
     wait(r_all.at[pl.ds(0, n_chip - 1)], send_sems.at[0])
     wait(rmid, send_sems.at[5])
@@ -292,6 +292,12 @@
 
     wait(precv.at[pl.ds(0, half - 1)], send_sems.at[2])
     wait(rrecv.at[pl.ds(0, n_chip - 1)], send_sems.at[3])
+
+
+def finish(rows_all, span, pair_ref, grad_ref, proj_ref, br_ref, pair_out, grad_out, proj_out):
+    pair_out[...] = pair_ref[...] * (1.0 / rows_all) + br_ref[...]
+    grad_out[...] = grad_ref[...]
+    proj_out[...] = proj_ref[...] * (1.0 / span)
 
 
 def solution(mesh):
@@ -317,7 +323,7 @@
                 jax.ShapeDtypeStruct((s_loc * tile_j, feats), f32),
                 jax.ShapeDtypeStruct((rp, pair_ch), f32),
             ),
-            in_specs=[pl.BlockSpec(memory_space=pltpu.VMEM)] * 10,
+            in_specs=[pl.BlockSpec(memory_space=pltpu.VMEM)] * 9,
             out_specs=(pl.BlockSpec(memory_space=pltpu.VMEM),) * 3,
             scratch_shapes=[
                 vm(feats // LANES, s_loc * tile_j, LANES),
@@ -353,9 +359,15 @@
             ),
         )(
             x.reshape(s_loc * tile_j, feats), scale.reshape(1, -1), offset.reshape(1, -1),
-            w1.T, b1.reshape(1, -1), w2.T, b2.reshape(1, -1), wr, br.reshape(1, -1),
+            w1.T, b1.reshape(1, -1), w2.T, b2.reshape(1, -1), wr,
             cot.reshape(tile_i * tile_j, pair_ch),
         )
+        pair, grad, proj = pl.pallas_call(
+            functools.partial(finish, rows_all, tile_j * n_col),
+            out_shape=tuple(jax.ShapeDtypeStruct(a.shape, f32) for a in (pair, grad, proj)),
+            in_specs=[pl.BlockSpec(memory_space=pltpu.VMEM)] * 4,
+            out_specs=(pl.BlockSpec(memory_space=pltpu.VMEM),) * 3,
+        )(pair, grad, proj, br.reshape(1, -1))
         return (
             pair.reshape(tile_i, tile_j, pair_ch),
             grad.reshape(s_loc, tile_j, feats),

time: 35.7 us -> 33.6 us (0.941)
  local copies, waits for them, and re-layouts: 3.77 us -> 0 us
  Pallas kernels: 31.1 us -> 32.8 us
    unnamed x5 -> x0, local copies, waits for them, and re-layouts: 3.77 us -> none
    pallas_call x0 -> x1, Pallas kernels: none -> 1.69 us  [local(): pl.pallas_call(functools.partial(finish, rows_all, tile_j * n_col), out_s...]
where the time goes in v3:
time: 33.6 us; the launch traced here: 33.4 us
  Pallas kernels  32.8 us (98%)
  between operations  0.64 us (2%)
    pallas_call x1, Pallas kernels, local(): pl.pallas_call(functools.partial(kernel, n_row, n_col, s_loc, tile_i, til...  31.1 us
    pallas_call x1, Pallas kernels, local(): pl.pallas_call(functools.partial(finish, rows_all, tile_j * n_col), out_s...  1.69 us

profile of v3, /device:TPU:24, one launch (start us, length us, event | category | flops | bytes accessed | tf_op | source)
XLA Modules:
  0.0 33.4 jit_solution(727273209284170160)
XLA Ops:
  0.6 31.1 %shard_map.121 = (f32[128,128]{1,0:T(8,128)}, f32[256,256]{1,0:T(8,128)}, f32[32,128]{1,0:T(8,128)}) custom-call(f32[256,256]{1,0:T(8,128)} %bitcast.11, f32[1,256]{1,0:T(1,128)} %bitcast.15, f32[1,256]{1,0:T(1,128)} %bitcast.16, f32[32,256]{1,0:T(8,128)} %bitcast.13, f32[1,32]{1,0:T(1,128)} %bitcast.17, f32[32,256]{1,0:T(8,128)} %bitcast.14, ...), custom_call_target="tpu_custom_call" | custom-call | tf_op jit(solution)/shard_map/pallas_call | solution.py:319
  31.7 1.7 %shard_map.122 = (f32[128,128]{1,0:T(8,128)}, f32[256,256]{1,0:T(8,128)}, f32[32,128]{1,0:T(8,128)}) custom-call(f32[128,128]{1,0:T(8,128)} %get-tuple-element.9.pair_ref, f32[256,256]{1,0:T(8,128)} %get-tuple-element.10.grad_ref, f32[32,128]{1,0:T(8,128)} %get-tuple-element.11.proj_ref, f32[1,128]{1,0:T(1,128)} %bitcast.19), custom_call_target="tpu_custom_call" | custom-call | tf_op jit(solution)/shard_map/pallas_call | solution.py:365
